TPU v7x, 32 devices: a whole 2x2x4 slice. The times are simulated.
32 devices in a mesh: task: 4 (over z), tile: 8 (over y, x, core).
Axes of the slice: x: 2, y: 2, z: 4, core: 2. Of those that a mesh axis runs over, the one named last changes fastest.
Arguments:
- adjusted: bfloat16 [8, 3584, 18944], P('task', 'tile'), may hold values from -6 to 6
- fisher: bfloat16 [8, 3584, 18944], P('task', 'tile'), may hold values from 0.0099487305 to 10
Outputs:
- merged: bfloat16 [3584, 18944], P(None, ('task', 'tile'))
All inputs are finite; a program needn't handle non-finite values.
Results may differ from a plain program's by a relative error of at most 0.001.
Values may be sent and summed in bfloat16 or wider, within the bound.
A program may use at most 256 MiB of HBM per device.

v0:
```python
import functools
import math
import jax
import jax.numpy as jnp
from jax import lax
from jax.experimental import pallas as pl
from jax.experimental.pallas import tpu as pltpu
from jax.sharding import PartitionSpec as P

MESH = pl.DeviceIdType.MESH
LANES = 128
LOW, HIGH = 0.0099487305, 10.0
ODD, POWER = 15, 24
LIFT = 2.0**8.25


def over(count, step, carry, unroll=4):
    def trip(i, value):
        for u in range(unroll):
            value = step(i * unroll + u, value)
        return value

    carry = lax.fori_loop(0, count // unroll, trip, carry)
    for j in range(count // unroll * unroll, count):
        carry = step(j, carry)
    return carry


def kernel(n, rows, width, adj, fis, out, from_left, from_right, loc_a, loc_f, wire, got, num, den,
           loc_sem, send_sem, left_sem, right_sem, got_sem):
    me = lax.axis_index("task")
    chunks = out.shape[0] // rows
    blocks = width // LANES
    per_device = adj.shape[0] * math.sqrt(LOW * HIGH)
    f32 = jnp.float32

    def lanes(j, base=0):
        return pl.ds(pl.multiple_of(base + j * LANES, LANES), LANES)

    def loads(s, q, c, slot):
        where = (slice(None), pl.ds(pl.multiple_of(c * rows, rows), rows), pl.ds(pl.multiple_of(q * width, LANES), width))
        return (
            pltpu.make_async_copy(adj.at[where], loc_a.at[s, slot], loc_sem.at[s, slot, 0]),
            pltpu.make_async_copy(fis.at[where], loc_f.at[s, slot], loc_sem.at[s, slot, 1]),
        )

    def sending(s, q, c, slot):
        inbox, sem, to = ((from_left, left_sem, me + 1), (from_right, right_sem, me - 1))[s]
        return pltpu.make_async_remote_copy(
            src_ref=wire.at[s, slot], dst_ref=inbox.at[q, c], send_sem=send_sem.at[s, slot],
            recv_sem=sem.at[q * chunks + c], device_id={"task": to}, device_id_type=MESH)

    def local(s, slot):
        def step(j, carry):
            f, a = loc_f[s, slot, :, :, lanes(j)].astype(f32), loc_a[s, slot, :, :, lanes(j)].astype(f32)
            num[:, lanes(j)] = jnp.sum(f * a, axis=0)
            den[:, lanes(j)] = jnp.sum(f, axis=0)
            return carry

        over(blocks, step, 0)

    def arrive(side, q, c, held):
        sending(side, q, c, 0).wait_recv()
        inbox = (from_left, from_right)[side]
        copy = pltpu.make_async_copy(inbox.at[q, c], got.at[side], got_sem.at[side])
        copy.start()
        copy.wait()
        centre = per_device * held.astype(f32)
        unit = got[side, :, 2 * width:2 * width + LANES].astype(f32) * (1.0 / LIFT)

        def step(j, carry):
            y = got[side, :, lanes(j)].astype(f32)
            d = jnp.exp2(jnp.log2(got[side, :, lanes(j, width)].astype(f32)) * (1.0 / POWER)) * centre
            size = jnp.exp2(jnp.log2(jnp.maximum(jnp.abs(y), 2.0**-126)) * (1.0 / ODD)) * unit
            r = jnp.where(y < 0, -size, jnp.where(y > 0, size, 0.0))
            num[:, lanes(j)] += r * d
            den[:, lanes(j)] += d
            return carry

        over(blocks, step, 0)

    def encode(s, slot, held):
        def ratio(j, top):
            r = num[:, lanes(j)] / den[:, lanes(j)]
            num[:, lanes(j)] = r
            return jnp.maximum(top, jnp.abs(r))

        top = over(blocks, ratio, jnp.zeros((rows, LANES), f32))
        top = jnp.max(top, axis=1, keepdims=True)
        scale = jnp.broadcast_to(jnp.maximum(top * 1.01, 1e-35), (rows, LANES)).astype(jnp.bfloat16)
        wire[s, slot, :, 2 * width:2 * width + LANES] = scale
        factor = LIFT / scale.astype(f32)
        inverse = 1.0 / (per_device * held.astype(f32))

        def step(j, carry):
            x = num[:, lanes(j)] * factor
            x2 = x * x
            x4 = x2 * x2
            x8 = x4 * x4
            wire[s, slot, :, lanes(j)] = ((x * x2) * (x4 * x8)).astype(jnp.bfloat16)
            v = den[:, lanes(j)] * inverse
            v2 = v * v
            v4 = v2 * v2
            v8 = v4 * v4
            wire[s, slot, :, lanes(j, width)] = (v8 * v8 * v8).astype(jnp.bfloat16)
            return carry

        over(blocks, step, 0)

    def finish(c):
        def step(j, carry):
            merged = num[:, lanes(j)] / den[:, lanes(j)]
            out[pl.ds(pl.multiple_of(c * rows, rows), rows), lanes(j)] = merged.astype(jnp.bfloat16)
            return carry

        over(blocks, step, 0)

    has_left, has_right = me > 0, me < n - 1
    barrier = pltpu.get_barrier_semaphore()
    for there, to in ((has_left, me - 1), (has_right, me + 1)):
        @pl.when(there)
        def _():
            pl.semaphore_signal(barrier, inc=1, device_id={"task": to}, device_id_type=MESH)
    pl.semaphore_wait(barrier, has_left.astype(jnp.int32) + has_right.astype(jnp.int32))

    lasts = ((n - 1 - me) * chunks, me * chunks, chunks)
    quarter = (lambda i: n - 1 - i // chunks, lambda i: i // chunks, lambda i: me)

    def begin(s, i):
        for copy in loads(s, quarter[s](i), i % chunks, i % 2):
            copy.start()

    def work(s, i):
        q, c, slot = quarter[s](i), i % chunks, i % 2

        @pl.when(i + 1 < lasts[s])
        def _():
            begin(s, i + 1)

        for copy in loads(s, q, c, slot):
            copy.wait()
        local(s, slot)
        if s != 1:
            @pl.when(has_left)
            def _():
                arrive(0, q, c, me)
        if s != 0:
            @pl.when(has_right)
            def _():
                arrive(1, q, c, n - 1 - me)
        if s == 2:
            finish(c)
            return

        @pl.when(i >= 2)
        def _():
            sending(s, q, c, slot).wait_send()

        encode(s, slot, (me + 1, n - me)[s])
        sending(s, q, c, slot).start()

    for s in range(2):
        @pl.when(lasts[s] > 0)
        def _():
            begin(s, 0)
    begin(2, 0)
    late = (n - 2) * chunks

    def trip(t, carry):
        for s in range(2):
            @pl.when(t < lasts[s])
            def _():
                work(s, t)

        @pl.when(t >= late)
        def _():
            work(2, t - late)
        return carry

    lax.fori_loop(0, late + chunks, trip, 0)
    for s in range(2):
        @pl.when(lasts[s] > 0)
        def _():
            for slot in range(2):
                sending(s, 0, 0, slot).wait_send()


def body(n, adjusted, fisher):
    models, height, columns = adjusted.shape
    width = columns // n
    rows = next(r for r in (32, 16, 8, height) if height % r == 0)
    chunks = height // rows
    bf16 = jnp.bfloat16
    line = 2 * width + LANES
    merged, _, _ = pl.pallas_call(
        functools.partial(kernel, n, rows, width),
        out_shape=(
            jax.ShapeDtypeStruct((height, width), bf16),
            jax.ShapeDtypeStruct((n, chunks, rows, line), bf16),
            jax.ShapeDtypeStruct((n, chunks, rows, line), bf16),
        ),
        in_specs=[pl.BlockSpec(memory_space=pl.ANY)] * 2,
        out_specs=(pl.BlockSpec(memory_space=pltpu.VMEM), pl.BlockSpec(memory_space=pl.ANY), pl.BlockSpec(memory_space=pl.ANY)),
        scratch_shapes=[
            pltpu.VMEM((3, 2, models, rows, width), bf16),
            pltpu.VMEM((3, 2, models, rows, width), bf16),
            pltpu.VMEM((2, 2, rows, line), bf16),
            pltpu.VMEM((2, rows, line), bf16),
            pltpu.VMEM((rows, width), jnp.float32),
            pltpu.VMEM((rows, width), jnp.float32),
            pltpu.SemaphoreType.DMA((3, 2, 2)),
            pltpu.SemaphoreType.DMA((2, 2)),
            pltpu.SemaphoreType.DMA((n * chunks,)),
            pltpu.SemaphoreType.DMA((n * chunks,)),
            pltpu.SemaphoreType.DMA((2,)),
        ],
        compiler_params=pltpu.CompilerParams(collective_id=0, has_side_effects=True, vmem_limit_bytes=60 * 1024 * 1024),
    )(adjusted, fisher)
    return lax.all_to_all(merged, "tile", split_axis=1, concat_axis=0, tiled=True)


def solution(mesh):
    return jax.shard_map(
        functools.partial(body, mesh.shape["task"]),
        mesh=mesh,
        in_specs=(P("task", "tile", None), P("task", "tile", None)),
        out_specs=P(None, ("task", "tile")),
        check_vma=False,
    )
```

profile of v0, /device:TPU:8, one launch (start us, length us, event | category | flops | bytes accessed | tf_op | source)
XLA Modules:
  0.0 726.4 jit_solution(7090876670345989861)
XLA Ops:
  0.0 650.2 %shard_map.28 = (bf16[448,4736]{1,0:T(8,128)(2,1)}, bf16[4,14,32,9600]{3,2,1,0:T(8,128)(2,1)}, bf16[4,14,32,9600]{3,2,1,0:T(8,128)(2,1)}) custom-call(bf16[2,448,18944]{2,1,0:T(8,128)(2,1)} %adj.1, bf16[2,448,18944]{2,1,0:T(8,128)(2,1)} %fis.1), custom_call_target="tpu_custom_call" | custom-call | tf_op jit(solution)/shard_map/pallas_call | solution.py:195
  650.2 9.4 %all_to_all.14 = bf16[448,8,592]{2,1,0:T(8,128)(2,1)} reshape(bf16[448,4736]{1,0:T(8,128)(2,1)} %get-tuple-element.6) | data formatting | bytes 8486912 | tf_op jit(solution)/shard_map/all_to_all | solution.py:219
  659.6 2.9 copy.4
  662.5 56.9 %all_to_all.19 = bf16[448,8,592]{2,0,1:T(8,128)(2,1)} all-to-all(bf16[448,8,592]{2,0,1:T(8,128)(2,1)S(1)} %copy.4), channel_id=1, replica_groups=mesh['task'=4,'tile'=8] {'tile'}, dimensions={1} | all-to-all | bytes 8486912 | tf_op jit(solution)/shard_map/all_to_all | solution.py:219
  719.4 7.1 copy.5
where the time goes:
time: 729 us; the launch traced here: 726 us
  Pallas kernels  650 us (89%)
  blocking collectives  56.9 us (8%)
  local copies, waits for them, and re-layouts  19.4 us (3%)
    pallas_call x1, Pallas kernels, body(): pl.pallas_call(functools.partial(kernel, n, rows, width), out_shape=(jax....  650 us
    all_to_all x1, blocking collectives, body(): lax.all_to_all(merged, 'tile', split_axis=1, concat_axis=0, tiled=True)  56.9 us
    all_to_all x3, local copies, waits for them, and re-layouts, body(): lax.all_to_all(merged, 'tile', split_axis=1, concat_axis=0, tiled=True)  19.4 us

commit v1 on v0

v1 whole, which is shorter than its diff:
```python
import functools
import math
import jax
import jax.numpy as jnp
from jax import lax
from jax.experimental import pallas as pl
from jax.experimental.pallas import tpu as pltpu
from jax.sharding import PartitionSpec as P

MESH = pl.DeviceIdType.MESH
LANES = 128
LOW, HIGH = 0.0099487305, 10.0
ODD, POWER = 15, 24
LIFT = 2.0**8.25
TINY = 2.0**-126
SLOTS = 4
SKEW = 2
LAG = 16
WIDE = 4


def over(width, step, carry):
    big = WIDE * LANES
    trips = width // big
    carry = lax.fori_loop(0, trips, lambda i, v: step(pl.multiple_of(i * big, big), big, v), carry)
    if width % big:
        carry = step(trips * big, width % big, carry)
    return carry


def spread(block, size):
    return jnp.concatenate([block] * (size // LANES), axis=1) if size > LANES else block


def kernel(n, tiles, rows, width, share, adj, fis, out, inbox, loc_a, loc_f, wire, stage, whole,
           loc_sem, send_sem, recv_sem, near_sem, far_sem, own_sem, out_sem):
    me, tile = lax.axis_index("task"), lax.axis_index("tile")
    f32, bf16 = jnp.float32, jnp.bfloat16
    models, height = adj.shape[0], adj.shape[1]
    chunks = height // rows
    half = n // 2
    count = half * chunks
    per_device = models * math.sqrt(LOW * HIGH)
    last = n - 1

    place = (me, last - me)

    def quarter(s, i):
        return half + i // chunks if s == 0 else half - 1 - i // chunks

    def loads(s, i):
        c, slot = lax.rem(i, chunks), lax.rem(i, 2)
        where = (slice(None), pl.ds(pl.multiple_of(c * rows, rows), rows),
                 pl.ds(pl.multiple_of(quarter(s, i) * width, LANES), width))
        return (
            pltpu.make_async_copy(adj.at[where], loc_a.at[s, slot], loc_sem.at[s, slot, 0]),
            pltpu.make_async_copy(fis.at[where], loc_f.at[s, slot], loc_sem.at[s, slot, 1]),
        )

    def sending(s, i):
        slot = lax.rem(i, SLOTS)
        return pltpu.make_async_remote_copy(
            src_ref=wire.at[s, slot], dst_ref=inbox.at[s, i], send_sem=send_sem.at[s, slot],
            recv_sem=recv_sem.at[s, i], device_id={"task": me + 1 if s == 0 else me - 1}, device_id_type=MESH)

    def local(s, slot, lo, size):
        num = den = None
        for m in range(models):
            f = loc_f[s, slot, m, :, pl.ds(lo, size)].astype(f32)
            fa = f * loc_a[s, slot, m, :, pl.ds(lo, size)].astype(f32)
            num, den = (fa, f) if m == 0 else (num + fa, den + f)
        return num, den

    def gathered(s, i, slot, lo, size, unit, centre):
        num, den = local(s, slot, lo, size)
        if unit is None:
            return num, den
        y = inbox[s, i, :, pl.ds(lo, size)].astype(f32)
        level = jnp.log2(inbox[s, i, :, pl.ds(width + lo, size)].astype(f32)) * (1.0 / POWER)
        size_of = jnp.log2(jnp.maximum(jnp.abs(y), TINY)) * (1.0 / ODD - 1.0)
        num = num + (y * jnp.exp2(size_of + level)) * spread(unit * centre, size)
        den = den + jnp.exp2(level) * centre
        return num, den

    def taken(s, i, first):
        if first:
            return None, None, None
        top = inbox[s, i, :, 2 * width:2 * width + LANES].astype(f32)
        return top, top * (1.0 / LIFT), per_device * place[s].astype(f32)

    def encode(s, i, first):
        slot, to = lax.rem(i, 2), lax.rem(i, SLOTS)
        top, unit, centre = taken(s, i, first)

        def peak(lo, size, high):
            for m in range(models):
                a = jnp.abs(loc_a[s, slot, m, :, pl.ds(lo, size)])
                for k in range(size // LANES):
                    high = jnp.maximum(high, a[:, k * LANES:(k + 1) * LANES].astype(f32))
            return high

        start = jnp.full((rows, LANES), 1e-35, f32) if first else top
        high = over(width, peak, start).astype(bf16)
        wire[s, to, :, 2 * width:2 * width + LANES] = high
        factor = LIFT / high.astype(f32)
        shift = -POWER * jnp.log2(per_device * (place[s] + 1).astype(f32))

        def step(lo, size, carry):
            num, den = gathered(s, i, slot, lo, size, unit, centre)
            log = jnp.log2(den)
            x = num * jnp.exp2(-log) * spread(factor, size)
            x2 = x * x
            x3 = x2 * x
            x6 = x3 * x3
            wire[s, to, :, pl.ds(lo, size)] = (x6 * x6 * x3).astype(bf16)
            wire[s, to, :, pl.ds(width + lo, size)] = jnp.exp2(log * POWER + shift).astype(bf16)
            return carry

        over(width, step, 0)

    def finish(s, i):
        slot = lax.rem(i, 2)
        _, unit, centre = taken(s, i, False)

        def step(lo, size, carry):
            num, den = gathered(s, i, slot, lo, size, unit, centre)
            whole[:, pl.ds(lo, size)] = (num / den).astype(bf16)
            return carry

        over(width, step, 0)
        for t in range(tiles):
            stage[i, t] = whole[:, t * share:(t + 1) * share]

    def place_of(i):
        return pl.ds(pl.multiple_of(tile * height + lax.rem(i, chunks) * rows, rows), rows)

    def hand_out(i, to_task, peer, sem):
        return pltpu.make_async_remote_copy(
            src_ref=stage.at[i, peer], dst_ref=out.at[place_of(i)], send_sem=sem, recv_sem=out_sem,
            device_id={"task": to_task, "tile": peer}, device_id_type=MESH)

    def keep(i):
        return pltpu.make_async_copy(stage.at[i, tile], out.at[place_of(i)], own_sem)

    def send_far(s, i):
        for o in range(tiles):
            hand_out(i, quarter(s, i), lax.rem(tile + o, tiles), far_sem).start()

    def send_near(i):
        keep(i).start()
        for o in range(1, tiles):
            hand_out(i, me, lax.rem(tile + o, tiles), near_sem).start()

    def begin(s, i):
        for copy in loads(s, i):
            copy.start()

    def work(s, i):
        @pl.when(i + 1 < count)
        def _():
            begin(s, i + 1)

        for copy in loads(s, i):
            copy.wait()

        @pl.when(jnp.logical_and(place[s] < last, i >= SLOTS))
        def _():
            sending(s, i).wait_send()

        @pl.when(place[s] == 0)
        def _():
            encode(s, i, True)

        @pl.when(place[s] > 0)
        def _():
            sending(s, i).wait_recv()

            @pl.when(place[s] < last)
            def _():
                encode(s, i, False)

            @pl.when(place[s] == last)
            def _():
                finish(s, i)

                @pl.when(i >= count - chunks)
                def _():
                    send_near(i)

        @pl.when(place[s] < last)
        def _():
            sending(s, i).start()

    far = count - chunks
    lag = min(LAG, far)
    begin_far = count + SKEW * last - far + lag

    for s in range(2):
        begin(s, 0)

    def trip(t, carry):
        for s in range(2):
            i = t - SKEW * place[s]

            @pl.when(jnp.logical_and(i >= 0, i < count))
            def _():
                work(s, i)

            @pl.when(jnp.logical_and(place[s] == last, t >= begin_far))
            def _():
                send_far(s, t - begin_far)
        return carry

    lax.fori_loop(0, count + SKEW * last, trip, 0)

    for s in range(2):
        @pl.when(place[s] == last)
        def _():
            def rest(i, carry):
                send_far(s, i)
                return carry

            lax.fori_loop(far - lag, far, rest, 0)

        @pl.when(place[s] < last)
        def _():
            for i in range(count - SLOTS, count):
                sending(s, i).wait_send()

    at_end = jnp.logical_or(me == 0, me == last)

    @pl.when(at_end)
    def _():
        gone = stage.at[pl.ds(0, far)]
        pltpu.make_async_copy(gone, gone, far_sem).wait()
        gone = stage.at[pl.ds(far, chunks), pl.ds(0, tiles - 1)]
        pltpu.make_async_copy(gone, gone, near_sem).wait()
        gone = stage.at[pl.ds(far, chunks), pl.ds(0, 1)]
        pltpu.make_async_copy(gone, gone, own_sem).wait()
        come = out.at[pl.ds(0, (tiles - 1) * height)]
        pltpu.make_async_copy(come, come, out_sem).wait()

    @pl.when(jnp.logical_not(at_end))
    def _():
        pltpu.make_async_copy(out, out, out_sem).wait()


def body(n, tiles, adjusted, fisher):
    models, height, columns = adjusted.shape
    width = columns // n
    share = width // tiles
    rows = next(r for r in (16, 8, height) if height % r == 0)
    chunks = height // rows
    count = n // 2 * chunks
    bf16 = jnp.bfloat16
    line = 2 * width + LANES
    dma = pltpu.SemaphoreType.DMA
    return pl.pallas_call(
        functools.partial(kernel, n, tiles, rows, width, share),
        out_shape=jax.ShapeDtypeStruct((tiles * height, share), bf16),
        in_specs=[pl.BlockSpec(memory_space=pl.ANY)] * 2,
        out_specs=pl.BlockSpec(memory_space=pl.ANY),
        scratch_shapes=[
            pltpu.VMEM((2, count, rows, line), bf16),
            pltpu.VMEM((2, 2, models, rows, width), bf16),
            pltpu.VMEM((2, 2, models, rows, width), bf16),
            pltpu.VMEM((2, SLOTS, rows, line), bf16),
            pltpu.VMEM((count, tiles, rows, share), bf16),
            pltpu.VMEM((rows, width), bf16),
            dma((2, 2, 2)),
            dma((2, SLOTS)),
            dma((2, count)),
            dma,
            dma,
            dma,
            dma,
        ],
        compiler_params=pltpu.CompilerParams(has_side_effects=True, vmem_limit_bytes=63 * 1024 * 1024),
    )(adjusted, fisher)


def solution(mesh):
    return jax.shard_map(
        functools.partial(body, mesh.shape["task"], mesh.shape["tile"]),
        mesh=mesh,
        in_specs=(P("task", "tile", None), P("task", "tile", None)),
        out_specs=P(None, ("task", "tile")),
        check_vma=False,
    )
```

time: 729 us -> 489 us (0.67)
  Pallas kernels: 650 us -> 481 us
  blocking collectives: 56.9 us -> 0 us
  local copies, waits for them, and re-layouts: 19.4 us -> 7.09 us
    pallas_call x1, Pallas kernels: 650 us -> 481 us  [body(): pl.pallas_call(functools.partial(kernel, n, tiles, rows, width, share), o...]
    all_to_all x1 -> x0, blocking collectives: 56.9 us -> none  [body(): lax.all_to_all(merged, 'tile', split_axis=1, concat_axis=0, tiled=True)]
    all_to_all x3 -> x0, local copies, waits for them, and re-layouts: 19.4 us -> none  [body(): lax.all_to_all(merged, 'tile', split_axis=1, concat_axis=0, tiled=True)]
where the time goes in v1:
time: 489 us; the launch traced here: 488 us
  Pallas kernels  481 us (98%)
  local copies, waits for them, and re-layouts  7.09 us (1%)
    pallas_call x1, Pallas kernels, body(): pl.pallas_call(functools.partial(kernel, n, tiles, rows, width, share), o...  481 us

profile of v1, /device:TPU:8, one launch (start us, length us, event | category | flops | bytes accessed | tf_op | source)
XLA Modules:
  0.0 488.1 jit_solution(11423114201196137986)
XLA Ops:
  0.0 481.0 %shard_map.28 = bf16[3584,592]{1,0:T(8,128)(2,1)} custom-call(bf16[2,448,18944]{2,1,0:T(8,128)(2,1)} %adj.1, bf16[2,448,18944]{2,1,0:T(8,128)(2,1)} %fis.1), custom_call_target="tpu_custom_call" | custom-call | tf_op jit(solution)/shard_map/pallas_call | solution.py:258
  481.0 7.1 %copy.3 = bf16[3584,592]{0,1:T(8,128)(2,1)} copy(bf16[3584,592]{1,0:T(8,128)(2,1)} %shard_map.28) | data formatting | bytes 8486912 | tf_op jit(solution)/shard_map/pallas_call | solution.py:258

commit v2 on v1

v2 whole, which is shorter than its diff:
```python
import functools
import math
import jax
import jax.numpy as jnp
from jax import lax
from jax.experimental import pallas as pl
from jax.experimental.pallas import tpu as pltpu
from jax.sharding import PartitionSpec as P

MESH = pl.DeviceIdType.MESH
LANES, FOLD = 128, 8
LOW, HIGH = 0.0099487305, 10.0
ODD, POWER = 15, 24
LIFT = 2.0**8.25
TINY = 2.0**-126
SLOTS = 2
SKEW = 4
EARLY = 16
WIDE = 4


def over(width, step, carry):
    big = WIDE * LANES
    trips = width // big
    carry = lax.fori_loop(0, trips, lambda i, v: step(pl.multiple_of(i * big, big), big, v), carry)
    if width % big:
        carry = step(trips * big, width % big, carry)
    return carry


def spread(block, rows, size):
    block = jnp.concatenate([block] * (rows // FOLD), axis=0) if rows > FOLD else block
    return jnp.concatenate([block] * (size // LANES), axis=1) if size > LANES else block


def streams(n, tiles, rows, width, adj, fis, inbox, tops, loc_a, loc_f, wire, high_out, loc_sem, send_sem, recv_sem, top_sems, finish, late):
    me = lax.axis_index("task")
    f32, bf16 = jnp.float32, jnp.bfloat16
    models, height = adj.shape[0], adj.shape[1]
    chunks = height // rows
    half, last = n // 2, n - 1
    count = half * chunks
    per_device = models * math.sqrt(LOW * HIGH)
    place = (me, last - me)
    turn = first_row(rows, height)

    def loads(s, i):
        q, slot = i // chunks, lax.rem(i, 2)
        column = half + q if s == 0 else half - 1 - q
        where = (slice(None), pl.ds(turn(lax.rem(i, chunks)), rows), pl.ds(pl.multiple_of(column * width, LANES), width))
        return (
            pltpu.make_async_copy(adj.at[where], loc_a.at[s, slot], loc_sem.at[s, slot, 0]),
            pltpu.make_async_copy(fis.at[where], loc_f.at[s, slot], loc_sem.at[s, slot, 1]),
        )

    def sending(s, i):
        slot, to = lax.rem(i, SLOTS), {"task": me + 1 if s == 0 else me - 1}
        return (
            pltpu.make_async_remote_copy(
                src_ref=high_out.at[s, slot], dst_ref=tops.at[s, i], send_sem=top_sems[0].at[s, slot],
                recv_sem=top_sems[1].at[s, i], device_id=to, device_id_type=MESH),
            pltpu.make_async_remote_copy(
                src_ref=wire.at[s, slot], dst_ref=inbox.at[s, i], send_sem=send_sem.at[s, slot],
                recv_sem=recv_sem.at[s, i], device_id=to, device_id_type=MESH),
        )

    def gathered(s, i, lo, size, unit, centre):
        slot = lax.rem(i, 2)
        num = den = None
        for m in range(models):
            f = loc_f[s, slot, m, :, pl.ds(lo, size)].astype(f32)
            fa = f * loc_a[s, slot, m, :, pl.ds(lo, size)].astype(f32)
            num, den = (fa, f) if m == 0 else (num + fa, den + f)
        if unit is None:
            return num, den
        y = inbox[s, i, :, pl.ds(lo, size)].astype(f32)
        level = jnp.log2(inbox[s, i, :, pl.ds(width + lo, size)].astype(f32)) * (1.0 / POWER)
        part = jnp.log2(jnp.maximum(jnp.abs(y), TINY)) * (1.0 / ODD - 1.0)
        num = num + (y * jnp.exp2(part + level)) * spread(unit * centre, rows, size)
        den = den + jnp.exp2(level) * centre
        return num, den

    def taken(s, i):
        top = tops[s, i].astype(f32)
        return top, top * (1.0 / LIFT), per_device * place[s].astype(f32)

    def encode(s, i, first):
        slot, to = lax.rem(i, 2), lax.rem(i, SLOTS)
        top, unit, centre = (jnp.full((FOLD, LANES), 1e-35, f32), None, None) if first else taken(s, i)

        def peak(lo, size, high):
            for m in range(models):
                a = jnp.abs(loc_a[s, slot, m, :, pl.ds(lo, size)].astype(f32))
                for k in range(size // LANES):
                    for h in range(rows // FOLD):
                        high = jnp.maximum(high, a[h * FOLD:(h + 1) * FOLD, k * LANES:(k + 1) * LANES])
            return high

        high = over(width, peak, top).astype(bf16)
        high_out[s, to] = high
        factor = LIFT / high.astype(f32)
        shift = -POWER * jnp.log2(per_device * (place[s] + 1).astype(f32))

        def step(lo, size, carry):
            num, den = gathered(s, i, lo, size, unit, centre)
            log = jnp.log2(den)
            x = num * jnp.exp2(-log) * spread(factor, rows, size)
            x2 = x * x
            x3 = x2 * x
            x6 = x3 * x3
            wire[s, to, :, pl.ds(lo, size)] = (x6 * x6 * x3).astype(bf16)
            wire[s, to, :, pl.ds(width + lo, size)] = jnp.exp2(log * POWER + shift).astype(bf16)
            return carry

        over(width, step, 0)

    def merge(s, i, put):
        _, unit, centre = taken(s, i)

        def step(lo, size, carry):
            num, den = gathered(s, i, lo, size, unit, centre)
            put(lo, size, (num / den).astype(bf16))
            return carry

        over(width, step, 0)

    def begin(s, i):
        for copy in loads(s, i):
            copy.start()

    def ready(s, i):
        @pl.when(i + 1 < count)
        def _():
            begin(s, i + 1)

        for copy in loads(s, i):
            copy.wait()

    def work(s, i):
        fresh = jnp.logical_or(i > 0, place[s] > 0)

        @pl.when(fresh)
        def _():
            ready(s, i)

        @pl.when(jnp.logical_and(place[s] < last, i >= SLOTS))
        def _():
            for copy in sending(s, i):
                copy.wait_send()

        @pl.when(jnp.logical_and(place[s] == 0, fresh))
        def _():
            encode(s, i, True)

        @pl.when(place[s] > 0)
        def _():
            for copy in sending(s, i):
                copy.wait_recv()

            @pl.when(place[s] < last)
            def _():
                encode(s, i, False)

            @pl.when(place[s] == last)
            def _():
                finish(s, i, functools.partial(merge, s, i))

        @pl.when(place[s] < last)
        def _():
            for copy in sending(s, i):
                copy.start()

    barrier = pltpu.get_barrier_semaphore()
    tile = lax.axis_index("tile")

    def greet(d, carry):
        there = {"task": d // tiles, "tile": lax.rem(d, tiles)}

        @pl.when(d != me * tiles + tile)
        def _():
            pl.semaphore_signal(barrier, inc=1, device_id=there, device_id_type=MESH)
        return carry

    lax.fori_loop(0, n * tiles, greet, 0)
    for s in range(2):
        begin(s, 0)

    for s in range(2):
        @pl.when(place[s] == 0)
        def _():
            ready(s, 0)
            encode(s, 0, True)

    pl.semaphore_wait(barrier, n * tiles - 1)

    def trip(t, carry):
        for s in range(2):
            i = t - SKEW * place[s]

            @pl.when(jnp.logical_and(i >= 0, i < count))
            def _():
                work(s, i)

            @pl.when(place[s] == last)
            def _():
                late(s, t)
        return carry

    trips = count + SKEW * last
    lax.fori_loop(0, trips, trip, 0)

    for s in range(2):
        @pl.when(place[s] == last)
        def _():
            late(s, None)

        @pl.when(place[s] < last)
        def _():
            for i in range(count - min(SLOTS, count), count):
                for copy in sending(s, i):
                    copy.wait_send()


def first_row(rows, height):
    if not shared(height):
        return lambda c: pl.multiple_of(c * rows, rows)
    lead = jnp.where(lax.rem(lax.axis_index("tile"), 2) == 0, height - LANES // 2, 0)
    return lambda c: pl.multiple_of(lax.rem(c * rows + lead, height), rows)


def shared(height):
    return height % LANES == LANES // 2


def flipped(n, tiles, rows, width, share, adj, fis, out, inbox, tops, loc_a, loc_f, wire, high_out, stage, group, pair,
            loc_sem, send_sem, recv_sem, top_send, top_recv, pair_sem, near_sem, far_sem, out_sem):
    me, tile = lax.axis_index("task"), lax.axis_index("tile")
    f32, bf16 = jnp.float32, jnp.bfloat16
    height = adj.shape[1]
    chunks, half = height // rows, n // 2
    middle = LANES // 2
    lead, per = middle // rows, LANES // rows
    full = height // LANES
    even = lax.rem(tile, 2) == 0
    first_block = (tile // 2) * (2 * full + 1)
    base = first_block + jnp.where(even, 0, full + 1)
    far = half - 1
    peers = tiles // 2
    first_peer = jnp.where(even, 0, peers)
    mine = (tile >= peers) != even
    strips = pl.cdiv(width // 2, LANES)
    first_strip = jnp.where(even, 0, width // LANES - strips)

    def column(slot):
        block = first_block + full if isinstance(slot, int) else base + slot
        return pl.ds(pl.multiple_of(block * LANES, LANES), LANES)

    def piece(q, slot, peer):
        return stage.at[q, slot, pl.ds(pl.multiple_of(peer * share, 8), share)]

    def handing(s, q, slot, peer, sem):
        return pltpu.make_async_remote_copy(
            src_ref=piece(q, slot, peer), dst_ref=out.at[:, column(slot)], send_sem=sem, recv_sem=out_sem,
            device_id={"task": half + q if s == 0 else half - 1 - q, "tile": peer}, device_id_type=MESH)

    def keep(slot):
        pltpu.make_async_copy(piece(far, slot, tile), out.at[:, column(slot)], out_sem).start()

    def near(s, slot):
        def one(o, carry):
            handing(s, far, slot, lax.rem(tile + o, tiles), near_sem.at[0]).start()
            return carry

        keep(slot)
        lax.fori_loop(1, tiles, one, 0)

    def near_pair(s):
        def one(o, carry):
            handing(s, far, full, first_peer + lax.rem(tile + o, peers), near_sem.at[1]).start()
            return carry

        pl.when(mine)(lambda: keep(full))
        lax.fori_loop(jnp.where(mine, 1, 0), peers, one, 0)

    def turn(q, slot, start, strips, get):
        def step(j, carry):
            at = pl.multiple_of((start + j) * LANES, LANES)
            stage[q, slot, pl.ds(at, LANES), :] = get(at).astype(f32).T.astype(bf16)
            return carry

        lax.fori_loop(0, strips, step, 0)

    def two_halves(q, at):
        own, other = group[pl.ds(LANES, middle), pl.ds(at, LANES)].astype(f32), pair[q, :, pl.ds(at, LANES)].astype(f32)
        return jnp.concatenate([jnp.where(even, own, other), jnp.where(even, other, own)], axis=0)

    def giving(q):
        return pltpu.make_async_remote_copy(
            src_ref=group.at[pl.ds(LANES, middle)], dst_ref=pair.at[q], send_sem=pair_sem.at[0], recv_sem=pair_sem.at[1 + q],
            device_id={"tile": tile + jnp.where(even, 1, -1)}, device_id_type=MESH)

    def finish(s, i, merge):
        q, c = i // chunks, lax.rem(i, chunks)
        at = pl.multiple_of(jnp.where(c < lead, LANES + c * rows, lax.rem(c - lead + per, per) * rows), rows)

        def put(lo, size, value):
            group[pl.ds(at, rows), pl.ds(lo, size)] = value

        merge(put)

        @pl.when(c == lead - 1)
        def _():
            giving(q).start()

        @pl.when(c == 2 * lead - 1)
        def _():
            giving(q).wait()
            turn(q, full, first_strip, strips, functools.partial(two_halves, q))

            @pl.when(q == far)
            def _():
                near_pair(s)

        @pl.when(jnp.logical_and(c >= lead, lax.rem(c - lead + per, per) == per - 1))
        def _():
            slot = (c - lead) // per
            turn(q, slot, 0, width // LANES, lambda at: group[pl.ds(0, LANES), pl.ds(at, LANES)])

            @pl.when(q == far)
            def _():
                near(s, slot)

    trips = half * chunks + SKEW * (n - 1)
    whole_blocks, early = far * full * tiles, min(EARLY, far * full * tiles)

    def far_block(s, p):
        handing(s, p // (full * tiles), lax.rem(p // tiles, full), lax.rem(tile + p, tiles), far_sem.at[0]).start()

    def late(s, t):
        if t is not None:
            @pl.when(t >= trips - early)
            def _():
                far_block(s, t - (trips - early))
            return

        def rest(p, carry):
            far_block(s, p)
            return carry

        lax.fori_loop(early, whole_blocks, rest, 0)

        def last_block(p, carry):
            handing(s, p // peers, full, first_peer + lax.rem(tile + p, peers), far_sem.at[1]).start()
            return carry

        lax.fori_loop(0, far * peers, last_block, 0)

    streams(n, tiles, rows, width, adj, fis, inbox, tops, loc_a, loc_f, wire, high_out, loc_sem, send_sem, recv_sem,
            (top_send, top_recv), finish, late)

    def settle(sem, blocks):
        if blocks:
            gone = out.at[:, pl.ds(0, blocks * LANES)]
            pltpu.make_async_copy(gone, gone, sem).wait()

    @pl.when(jnp.logical_or(me == 0, me == n - 1))
    def _():
        settle(near_sem.at[0], full * (tiles - 1))
        settle(far_sem.at[0], whole_blocks)

        settle(far_sem.at[1], far * peers)
        pl.when(mine)(lambda: settle(near_sem.at[1], peers - 1))
        pl.when(jnp.logical_not(mine))(lambda: settle(near_sem.at[1], peers))

    pltpu.make_async_copy(out, out, out_sem).wait()


def plain(n, tiles, rows, width, share, adj, fis, out, inbox, tops, loc_a, loc_f, wire, high_out, stage, whole,
          loc_sem, send_sem, recv_sem, top_send, top_recv, near_sem, far_sem, out_sem):
    me, tile = lax.axis_index("task"), lax.axis_index("tile")
    height = adj.shape[1]
    chunks, half = height // rows, n // 2
    far = (half - 1) * chunks

    def place_of(i):
        return pl.ds(pl.multiple_of(tile * height + lax.rem(i, chunks) * rows, rows), rows)

    def handing(s, i, peer, sem):
        q = i // chunks
        return pltpu.make_async_remote_copy(
            src_ref=stage.at[i, peer], dst_ref=out.at[place_of(i)], send_sem=sem, recv_sem=out_sem,
            device_id={"task": half + q if s == 0 else half - 1 - q, "tile": peer}, device_id_type=MESH)

    def finish(s, i, merge):
        def put(lo, size, value):
            whole[:, pl.ds(lo, size)] = value

        merge(put)
        for t in range(tiles):
            stage[i, t] = whole[:, t * share:(t + 1) * share]

        @pl.when(i >= far)
        def _():
            pltpu.make_async_copy(stage.at[i, tile], out.at[place_of(i)], out_sem).start()

            def one(o, carry):
                handing(s, i, lax.rem(tile + o, tiles), near_sem).start()
                return carry

            lax.fori_loop(1, tiles, one, 0)

    def late(s, t):
        if t is None:
            def rest(p, carry):
                handing(s, p // tiles, lax.rem(tile + p, tiles), far_sem).start()
                return carry

            lax.fori_loop(0, far * tiles, rest, 0)

    streams(n, tiles, rows, width, adj, fis, inbox, tops, loc_a, loc_f, wire, high_out, loc_sem, send_sem, recv_sem,
            (top_send, top_recv), finish, late)

    @pl.when(jnp.logical_or(me == 0, me == n - 1))
    def _():
        gone = out.at[pl.ds(0, (tiles - 1) * height)]
        pltpu.make_async_copy(gone, gone, near_sem).wait()
        if far:
            gone = stage.at[pl.ds(0, far)]
            pltpu.make_async_copy(gone, gone, far_sem).wait()

    pltpu.make_async_copy(out, out, out_sem).wait()


def body(n, tiles, adjusted, fisher):
    models, height, columns = adjusted.shape
    width = columns // n
    share = width // tiles
    flip = shared(height) and tiles % 2 == 0 and share % 8 == 0
    rows = next(r for r in (16, 8, height) if height % r == 0)
    half, chunks = n // 2, height // rows
    count = half * chunks
    bf16 = jnp.bfloat16
    dma = pltpu.SemaphoreType.DMA
    if flip:
        hold = [
            pltpu.VMEM((half, height // LANES + 1, width, LANES), bf16),
            pltpu.VMEM((LANES + LANES // 2, width), bf16),
            pltpu.VMEM((half, LANES // 2, width), bf16),
        ]
        ends = [dma((1 + half,)), dma((2,)), dma((2,)), dma]
    else:
        hold = [pltpu.VMEM((count, tiles, rows, share), bf16), pltpu.VMEM((rows, width), bf16)]
        ends = [dma, dma, dma]
    out = (share, tiles * height) if flip else (tiles * height, share)
    merged = pl.pallas_call(
        functools.partial(flipped if flip else plain, n, tiles, rows, width, share),
        out_shape=pltpu.VMEM(out, bf16),
        in_specs=[pl.BlockSpec(memory_space=pl.ANY)] * 2,
        out_specs=pl.BlockSpec(memory_space=pl.ANY),
        scratch_shapes=[
            pltpu.VMEM((2, count, rows, 2 * width), bf16),
            pltpu.VMEM((2, count, FOLD, LANES), bf16),
            pltpu.VMEM((2, 2, models, rows, width), bf16),
            pltpu.VMEM((2, 2, models, rows, width), bf16),
            pltpu.VMEM((2, SLOTS, rows, 2 * width), bf16),
            pltpu.VMEM((2, SLOTS, FOLD, LANES), bf16),
            *hold,
            dma((2, 2, 2)),
            dma((2, SLOTS)),
            dma((2, count)),
            dma((2, SLOTS)),
            dma((2, count)),
            *ends,
        ],
        compiler_params=pltpu.CompilerParams(collective_id=0, has_side_effects=True, vmem_limit_bytes=53 * 1024 * 1024),
    )(adjusted, fisher)
    return merged.T if flip else merged


def solution(mesh):
    return jax.shard_map(
        functools.partial(body, mesh.shape["task"], mesh.shape["tile"]),
        mesh=mesh,
        in_specs=(P("task", "tile", None), P("task", "tile", None)),
        out_specs=P(None, ("task", "tile")),
        check_vma=False,
    )
```

time: 489 us -> 470 us (0.961)
  Pallas kernels: 481 us -> 466 us
  local copies, waits for them, and re-layouts: 7.09 us -> 2.03 us
    pallas_call x1, Pallas kernels: 481 us -> 466 us  [body(): pl.pallas_call(functools.partial(flipped if flip else plain, n, tiles, ro...]
    pallas_call x1 -> x0, local copies, waits for them, and re-layouts: 7.09 us -> none  [body(): pl.pallas_call(functools.partial(kernel, n, tiles, rows, width, share), o...]
where the time goes in v2:
time: 470 us; the launch traced here: 468 us
  Pallas kernels  466 us (99%)
    pallas_call x1, Pallas kernels, body(): pl.pallas_call(functools.partial(flipped if flip else plain, n, tiles, ro...  466 us

profile of v2, /device:TPU:8, one launch (start us, length us, event | category | flops | bytes accessed | tf_op | source)
XLA Modules:
  0.0 467.9 jit_solution(4541850109806374070)
XLA Ops:
  0.0 465.9 %shard_map.28 = bf16[592,3584]{1,0:T(8,128)(2,1)S(1)} custom-call(bf16[2,448,18944]{2,1,0:T(8,128)(2,1)} %adj.1, bf16[2,448,18944]{2,1,0:T(8,128)(2,1)} %fis.1), custom_call_target="tpu_custom_call" | custom-call | tf_op jit(solution)/shard_map/pallas_call | solution.py:455
  465.9 2.0 copy.4

commit v3 on v2

--- a/solution.py
+++ b/solution.py
@@ -81,7 +81,7 @@
         return num, den
 
     def taken(s, i):
-        top = tops[s, i].astype(f32)
+        top = jnp.broadcast_to(tops[s, i], (FOLD, LANES))
         return top, top * (1.0 / LIFT), per_device * place[s].astype(f32)
 
     def encode(s, i, first):
@@ -96,9 +96,9 @@
                         high = jnp.maximum(high, a[h * FOLD:(h + 1) * FOLD, k * LANES:(k + 1) * LANES])
             return high
 
-        high = over(width, peak, top).astype(bf16)
+        high = jnp.max(over(width, peak, top), axis=0, keepdims=True)
         high_out[s, to] = high
-        factor = LIFT / high.astype(f32)
+        factor = jnp.broadcast_to(LIFT / high, (FOLD, LANES))
         shift = -POWER * jnp.log2(per_device * (place[s] + 1).astype(f32))
 
         def step(lo, size, carry):
@@ -173,17 +173,25 @@
     barrier = pltpu.get_barrier_semaphore()
     tile = lax.axis_index("tile")
 
+    first_task = (me // half) * half
+    across = jnp.logical_or(me == half - 1, me == half)
+
     def greet(d, carry):
-        there = {"task": d // tiles, "tile": lax.rem(d, tiles)}
-
-        @pl.when(d != me * tiles + tile)
+        there = {"task": first_task + d // tiles, "tile": lax.rem(d, tiles)}
+
+        @pl.when(d != (me - first_task) * tiles + tile)
         def _():
             pl.semaphore_signal(barrier, inc=1, device_id=there, device_id_type=MESH)
         return carry
 
-    lax.fori_loop(0, n * tiles, greet, 0)
     for s in range(2):
         begin(s, 0)
+    @pl.when(across)
+    def _():
+        pl.semaphore_signal(
+            barrier, inc=1, device_id={"task": jnp.where(me < half, half, half - 1)}, device_id_type=MESH)
+
+    lax.fori_loop(0, half * tiles, greet, 0)
 
     for s in range(2):
         @pl.when(place[s] == 0)
@@ -191,7 +199,7 @@
             ready(s, 0)
             encode(s, 0, True)
 
-    pl.semaphore_wait(barrier, n * tiles - 1)
+    pl.semaphore_wait(barrier, half * tiles - 1 + across.astype(jnp.int32))
 
     def trip(t, carry):
         for s in range(2):
@@ -459,11 +467,11 @@
         out_specs=pl.BlockSpec(memory_space=pl.ANY),
         scratch_shapes=[
             pltpu.VMEM((2, count, rows, 2 * width), bf16),
-            pltpu.VMEM((2, count, FOLD, LANES), bf16),
+            pltpu.VMEM((2, count, 1, LANES), jnp.float32),
             pltpu.VMEM((2, 2, models, rows, width), bf16),
             pltpu.VMEM((2, 2, models, rows, width), bf16),
             pltpu.VMEM((2, SLOTS, rows, 2 * width), bf16),
-            pltpu.VMEM((2, SLOTS, FOLD, LANES), bf16),
+            pltpu.VMEM((2, SLOTS, 1, LANES), jnp.float32),
             *hold,
             dma((2, 2, 2)),
             dma((2, SLOTS)),

time: 470 us -> 466 us (level)
  no operation moved by 1% of the time
where the time goes in v3:
time: 466 us; the launch traced here: 464 us
  Pallas kernels  462 us (99%)
    pallas_call x1, Pallas kernels, body(): pl.pallas_call(functools.partial(flipped if flip else plain, n, tiles, ro...  462 us

profile of v3, /device:TPU:8, one launch (start us, length us, event | category | flops | bytes accessed | tf_op | source)
XLA Modules:
  0.0 463.9 jit_solution(7344826841173341893)
XLA Ops:
  0.0 461.9 %shard_map.28 = bf16[592,3584]{1,0:T(8,128)(2,1)S(1)} custom-call(bf16[2,448,18944]{2,1,0:T(8,128)(2,1)} %adj.1, bf16[2,448,18944]{2,1,0:T(8,128)(2,1)} %fis.1), custom_call_target="tpu_custom_call" | custom-call | tf_op jit(solution)/shard_map/pallas_call | solution.py:463
  461.9 2.0 copy.4
